TPU v7x, 32 devices: a whole 2x2x4 slice. The times are simulated.
32 devices in a mesh: dp: 8 (over y, x, core), tensor: 4 (over z).
Axes of the slice: x: 2, y: 2, z: 4, core: 2. Of those that a mesh axis runs over, the one named last changes fastest.
Arguments:
- tokens: bfloat16 [16384, 768], P(('dp', 'tensor')), may hold values from -6 to 6
- segments: int32 [16384], P('dp'), may hold values from -1 to 9, as said below
- cotangent: bfloat16 [16384, 768], P(('dp', 'tensor')), may hold values from -6 to 6
- ln1_gain: bfloat16 [768], replicated, may hold values from 0.5 to 1.5
- ln1_bias: bfloat16 [768], replicated, may hold values from -2 to 2
- w_qkv: bfloat16 [768, 2304], P(None, 'tensor'), may hold values from -0.21875 to 0.21875
- q_bias: bfloat16 [768], P('tensor'), may hold values from -3 to 3
- v_bias: bfloat16 [768], P('tensor'), may hold values from -3 to 3
- w_out: bfloat16 [768, 768], P('tensor'), may hold values from -0.625 to 0.625
- out_bias: bfloat16 [768], replicated, may hold values from -2 to 2
- ln2_gain: bfloat16 [768], replicated, may hold values from 0.5 to 1.5
- ln2_bias: bfloat16 [768], replicated, may hold values from -2 to 2
- w_fc1: bfloat16 [768, 3072], P(None, 'tensor'), may hold values from -0.21875 to 0.21875
- fc1_bias: bfloat16 [3072], P('tensor'), may hold values from -3 to 3
- w_fc2: bfloat16 [3072, 768], P('tensor'), may hold values from -0.109375 to 0.109375
- fc2_bias: bfloat16 [768], replicated, may hold values from -2 to 2
Outputs:
- output: bfloat16 [16384, 768], P(('dp', 'tensor'))
- grad_tokens: bfloat16 [16384, 768], P(('dp', 'tensor'))
- cls_features: float32 [16384, 768], P(('dp', 'tensor'))
- grad_w_qkv: float32 [768, 2304], P('dp', 'tensor')
- grad_q_bias: float32 [768], replicated
- grad_v_bias: float32 [768], replicated
- grad_w_out: float32 [768, 768], P('tensor', 'dp')
- grad_out_bias: float32 [768], replicated
- grad_w_fc1: float32 [768, 3072], P('dp', 'tensor')
- grad_fc1_bias: float32 [3072], replicated
- grad_w_fc2: float32 [3072, 768], P('tensor', 'dp')
- grad_fc2_bias: float32 [768], replicated
- grad_ln1_gain: float32 [768], replicated
- grad_ln1_bias: float32 [768], replicated
- grad_ln2_gain: float32 [768], replicated
- grad_ln2_bias: float32 [768], replicated
Inputs may be any that keep to these rules, and one draw needn't show every extreme that they name: `segments`: within each aligned block of 512 positions the ids run 0, 1, 2, ... in order, id i over a run of 1 + 49 v positions with v from 1 to 4, starting at the block's first position; positions after the block's last whole sample hold -1. The first block begins with a run of 197; the last block holds only runs of 50, as many as fit.
All inputs are finite; a program needn't handle non-finite values.
Results may differ from a plain program's by a relative error of at most 0.024.
Values may be sent and summed in bfloat16 or wider, within the bound.
A program may use at most 128 MiB of HBM per device.

v0:
```python
from functools import partial
import math

import jax
import jax.numpy as jnp
from jax import lax
from jax.experimental import pallas as pl
from jax.experimental.pallas import tpu as pltpu
from jax.sharding import PartitionSpec as P

HD = 64
SEQ = 512
FAN = 8
F32 = jnp.float32
BF16 = jnp.bfloat16
MESH = pl.DeviceIdType.MESH
ANY = pl.BlockSpec(memory_space=pl.ANY)
VMEM = pl.BlockSpec(memory_space=pltpu.VMEM)


def mm(a, b):
    return lax.dot_general(a, b, (((1,), (0,)), ((), ())), preferred_element_type=F32)


def mm_nt(a, b):
    return lax.dot_general(a, b, (((1,), (1,)), ((), ())), preferred_element_type=F32)


def mm_tn(a, b):
    return lax.dot_general(a, b, (((0,), (0,)), ((), ())), preferred_element_type=F32)


class Place:
    def __init__(self, dp_size, parts):
        self.d = lax.axis_index("dp")
        self.t = lax.axis_index("tensor")
        self.dp_size, self.parts = dp_size, parts
        self.low = dp_size // FAN
        block = self.d // self.low
        self.y, self.x, self.c = block // 4, (block // 2) % 2, block % 2

    def flip(self, name):
        stride = self.low * {"y": 4, "x": 2, "c": 1}[name]
        bit = {"y": self.y, "x": self.x, "c": self.c}[name]
        return (self.d + stride * (1 - 2 * bit), self.t)

    def flip_stride(self, stride):
        bit = (self.d // stride) % 2
        return (self.d + stride * (1 - 2 * bit), self.t)

    def shift(self, k):
        return (self.d, (self.t + k) % self.parts)


def greet(partners):
    barrier = pltpu.get_barrier_semaphore()
    for partner in partners:
        pl.semaphore_signal(barrier, inc=1, device_id=partner, device_id_type=MESH)
    pl.semaphore_wait(barrier, len(partners))


class Link:
    def __init__(self, send_sem, recv_sem):
        self.send_sem, self.recv_sem, self.used = send_sem, recv_sem, 0

    def copy(self, src, dst, device):
        made = pltpu.make_async_remote_copy(
            src_ref=src,
            dst_ref=dst,
            send_sem=self.send_sem.at[self.used],
            recv_sem=self.recv_sem.at[self.used],
            device_id=device,
            device_id_type=MESH,
        )
        self.used += 1
        return made


def start(copies):
    for made in copies:
        made.start()


def arrive(copies):
    for made in copies:
        made.wait_recv()


def left(copies):
    for made in copies:
        made.wait_send()


def loop(count, body, hooks=None):
    def step(i, carry):
        for at, hook in (hooks or {}).items():
            pl.when(i == at)(hook)
        body(i)
        return carry

    lax.fori_loop(0, count, step, 0)


def add_into(target, other, lead):
    shape = other.shape[:lead]

    def body(i):
        index = []
        for extent in reversed(shape):
            index.append(i % extent)
            i = i // extent
        index = tuple(reversed(index))
        target_i, other_i = target.at[index], other.at[index]
        target_i[...] = (target_i[...].astype(F32) + other_i[...].astype(F32)).astype(target.dtype)

    loop(math.prod(shape), body)


def gather_unit(here, link, shard, whole):
    parts = here.parts
    y, x, c = here.y, here.x, here.c
    away = pl.ds(1, parts - 1)
    half = whole.shape[4] // 2
    lo, hi = pl.ds(0, half), pl.ds(half, half)
    along = [
        link.copy(shard.at[y, x, c], whole.at[parts - k, y, x, c], here.shift(k))
        for k in range(1, parts)
    ]
    a, b = whole.at[away, y, x, c, lo], whole.at[away, y, x, c, hi]
    first = [link.copy(a, a, here.flip("x")), link.copy(b, b, here.flip("y"))]
    a, b = whole.at[away, y, :, c, lo], whole.at[away, :, x, c, hi]
    second = [link.copy(a, a, here.flip("y")), link.copy(b, b, here.flip("x"))]
    a = whole.at[away, :, :, c]
    third = [link.copy(a, a, here.flip("c"))]
    return [along, first, second, third]


class Reduction:
    def __init__(self, here, link, grad, first, many, got, got_z):
        self.here, self.got = here, got
        got_c, got_y1, got_x2, got_x1, got_y2 = got
        y, x, c = here.y, here.x, here.c
        half = grad.shape[4] // 2
        self.lo, self.hi = lo, hi = pl.ds(0, half), pl.ds(half, half)
        self.grad = g = grad.at[pl.ds(first, many)]
        self.stages = [
            [link.copy(g.at[:, :, :, 1 - c], got_c, here.flip("c"))],
            [
                link.copy(g.at[:, 1 - y, :, c, lo], got_y1, here.flip("y")),
                link.copy(g.at[:, :, 1 - x, c, hi], got_x1, here.flip("x")),
            ],
            [
                link.copy(g.at[:, y, 1 - x, c, lo], got_x2, here.flip("x")),
                link.copy(g.at[:, 1 - y, x, c, hi], got_y2, here.flip("y")),
            ],
            [
                link.copy(grad.at[k, y, x, c], got_z.at[k - 1], here.shift(k))
                for k in range(first, first + many)
                if k > 0
            ],
        ]

    def step(self, s):
        y, x, c = self.here.y, self.here.x, self.here.c
        g, lo, hi = self.grad, self.lo, self.hi
        got_c, got_y1, got_x2, got_x1, got_y2 = self.got
        if s > 0:
            arrive(self.stages[s - 1])
        if s == 1:
            add_into(g.at[:, :, :, c], got_c, 3)
        if s == 2:
            add_into(g.at[:, y, :, c, lo], got_y1, 2)
            add_into(g.at[:, :, x, c, hi], got_x1, 2)
        if s == 3:
            add_into(g.at[:, y, x, c, lo], got_x2, 1)
            add_into(g.at[:, y, x, c, hi], got_y2, 1)
        if s < 4:
            start(self.stages[s])

    def drain(self):
        for copies in self.stages:
            left(copies)


def normalize(values):
    average = jnp.mean(values, axis=-1, keepdims=True)
    centered = values - average
    spread = jnp.mean(centered * centered, axis=-1, keepdims=True)
    scale = lax.rsqrt(spread + 1e-06)
    return centered * scale, scale


def normalize_back(hat, scale, gain, grad):
    scaled = grad * gain
    return (
        scaled
        - jnp.mean(scaled, axis=-1, keepdims=True)
        - hat * jnp.mean(scaled * hat, axis=-1, keepdims=True)
    ) * scale


ROWS = 64
UNITS = 5
NAMES = (
    "tokens",
    "cot",
    "segments",
    "vecs",
    "bias",
    "w_qkv",
    "w_out",
    "w_fc1",
    "w_fc2",
)
OUTS = (
    "output",
    "g_tokens",
    "s_qkv",
    "s_out",
    "s_fc1",
    "s_fc2",
    "small",
    "late",
    "cls",
)
SCRATCH = (
    "f_qkv",
    "f_out",
    "f_fc1",
    "f_fc2",
    "biases",
    "normed",
    "mixed",
    "mask",
    "lse",
    "heads",
    "resid",
    "normed2",
    "active",
    "slope",
    "turned",
    "acc",
    "tile",
    "g_low",
    "g_heads",
    "g_fc2",
    "g_out",
    "cols",
    "sums",
    "got_small",
    "late_sums",
    "got_late",
)


def layer_kernel(dp_size, parts, heads, *refs):
    refs = list(refs)
    ref = {}
    for name in NAMES + OUTS + SCRATCH:
        ref[name] = refs.pop(0)
    got = [[refs.pop(0) for _ in range(5)] for _ in range(UNITS + parts)]
    got_z = [refs.pop(0) for _ in range(UNITS + 1)]
    local_sem, send_sem, recv_sem = refs
    tokens, cot, cols, vecs = ref["tokens"], ref["cot"], ref["cols"], ref["vecs"]
    segments = ref["segments"]
    f_qkv, f_out, f_fc1, f_fc2 = ref["f_qkv"], ref["f_out"], ref["f_fc1"], ref["f_fc2"]
    biases, normed, mixed, mask = ref["biases"], ref["normed"], ref["mixed"], ref["mask"]
    lse, hd, resid, normed2 = ref["lse"], ref["heads"], ref["resid"], ref["normed2"]
    active, slope, turned, acc = ref["active"], ref["slope"], ref["turned"], ref["acc"]
    tile, g_low, g_heads, sums = ref["tile"], ref["g_low"], ref["g_heads"], ref["sums"]
    g_fc2, g_out = ref["g_fc2"], ref["g_out"]
    g_mixed = active
    wide = f_qkv.shape[5]
    g_qkv = f_fc1.at[:, :, :, :, :, pl.ds(0, wide)]
    g_fc1 = f_fc2
    width = tokens.shape[1]
    small, late = sums.at[0], ref["late_sums"].at[0]
    here = Place(dp_size, parts)
    qk_wide = heads * 128
    strides = [1 << b for b in range(dp_size.bit_length() - 1)]
    bits = [here.flip_stride(s) for s in strides]
    link = Link(send_sem, recv_sem)

    shards = [ref[n] for n in ("w_qkv", "w_out", "w_fc1", "w_fc2")]
    wholes = [f_qkv, f_out, f_fc1, f_fc2]
    own = [
        pltpu.make_async_copy(a, b.at[0], local_sem.at[i])
        for i, (a, b) in enumerate(zip(shards + [ref["bias"]], wholes + [biases]))
    ]
    start(own)
    greet(bits + [here.shift(k) for k in range(1, parts)])
    def columns(array, first, many):
        return array.at[:, :, :, :, pl.ds(first, many)] if len(array.shape) == 5 else array.at[:, :, :, :, :, pl.ds(first, many)]

    cut = f_fc1.shape[5] // 2
    plans = {"q": gather_unit(here, link, shards[0], f_qkv), "o": gather_unit(here, link, shards[1], f_out)}
    for name, i, first in (("a", 2, 0), ("b", 2, cut), ("c", 3, 0), ("d", 3, cut)):
        plans[name] = gather_unit(
            here, link, columns(shards[i], first, cut), columns(wholes[i], first, cut)
        )
    plans["q"][0] += [
        link.copy(ref["bias"], biases.at[parts - k], here.shift(k)) for k in range(1, parts)
    ]
    for plan in plans.values():
        start(plan[0])
    units = {}
    for i, (name, grad) in enumerate(
        (
            ("A", columns(g_fc2, 0, cut)),
            ("B", columns(g_fc2, cut, cut)),
            ("C", columns(g_fc1, 0, cut)),
            ("D", columns(g_fc1, cut, cut)),
            ("O", g_out),
        )
    ):
        units[name] = Reduction(here, link, grad, 0, parts, got[i], got_z[i])
    for k in range(parts):
        units[k] = Reduction(here, link, g_qkv, k, 1, got[UNITS + k], got_z[UNITS])

    def fwd(*steps):
        def run():
            for name, s in steps:
                arrive(plans[name][s])
                if s < 3:
                    start(plans[name][s + 1])

        return run

    def red(*steps):
        def run():
            for name, s in steps:
                units[name].step(s)

        return run

    def total(grad, got_last, out):
        value = grad[0, here.y, here.x, here.c].astype(F32)
        for k in range(parts - 1):
            value += got_last[k].astype(F32)
        out[...] = value

    tensor_bits = [
        (here.d, here.t + (1 << b) * (1 - 2 * ((here.t // (1 << b)) % 2)))
        for b in range(parts.bit_length() - 1)
    ]

    def butterfly(slots, got_slots):
        trips = [
            link.copy(slots.at[r], got_slots.at[r], partner)
            for r, partner in enumerate(bits + tensor_bits)
        ]

        def run(r):
            if r > 0:
                arrive([trips[r - 1]])
                slots[r] = slots[r - 1] + got_slots[r - 1]
            if r < len(trips):
                start([trips[r]])

        return trips, run

    trips, early_round = butterfly(sums, ref["got_small"])
    late_trips, late_round = butterfly(ref["late_sums"], ref["got_late"])

    def gain(i):
        return vecs[pl.ds(i, 1), :]

    chunks = SEQ // ROWS

    def rows_of(i):
        return pl.ds(pl.multiple_of(i * ROWS, ROWS), ROWS)

    small[...] = jnp.zeros_like(small)
    late[...] = jnp.zeros_like(late)
    labels = segments[pl.ds(here.t, 1), :]
    spot = lax.broadcasted_iota(jnp.int32, (1, SEQ), 1)
    earlier = pltpu.roll(labels, 1, 1)
    begins = (labels >= 0) & ((spot == 0) | (labels != earlier))
    line = labels.astype(F32)
    kinds = lax.broadcasted_iota(jnp.int32, (8, SEQ), 0)
    stacked = jnp.where(kinds == 0, line, jnp.where(kinds == 1, (labels >= 0).astype(F32), begins.astype(F32)))
    cols[...] = stacked.T

    def norm_one(i):
        r = rows_of(i)
        hat, _ = normalize(tokens[r, :].astype(F32))
        normed[r, :] = (hat * gain(0) + gain(1)).astype(BF16)
        mask[r, :] = jnp.where(cols[r, 0:1] == line, 0.0, -1e30)

    loop(chunks, norm_one)

    low_half = lax.broadcasted_iota(jnp.int32, (SEQ, 128), 1) < 64

    def qkv_part(k):
        for at in range(0, wide, 256):
            size = min(256, wide - at)
            w = f_qkv[k, :, :, :, :, pl.ds(at, size)].reshape(width, size)
            out = mm(normed[...], w) + biases[k, 0:1, pl.ds(at, size)].astype(F32)
            mixed[k, :, pl.ds(at, size)] = out.astype(BF16)

    def head_place(i):
        k, j = i // heads, i % heads
        at = pl.ds(pl.multiple_of(j * 128, 128), 128)
        v_at = pl.ds(pl.multiple_of(qk_wide + (j // 2) * 128, 128), 128)
        h_at = pl.ds(pl.multiple_of((j // 2) * 128, 128), 128)
        even = j % 2 == 0
        return k, at, v_at, h_at, even

    def scores_of(k, at):
        qk = mixed[k, :, at].astype(F32)
        q = jnp.where(low_half, qk * (1.0 / math.sqrt(HD)), 0.0).astype(BF16)
        kq = pltpu.roll(qk, 64, 1).astype(BF16)
        return mm_nt(kq, q) + mask[...], kq

    def mine_of(even):
        return low_half == even

    def attend(i):
        k, at, v_at, h_at, even = head_place(i)
        scores, _ = scores_of(k, at)
        highest = jnp.max(scores, axis=0, keepdims=True)
        expon = jnp.exp(scores - highest)
        total = jnp.sum(expon, axis=0, keepdims=True)
        lse[i, 0:1, :] = highest + jnp.log(total)
        weights = (expon * (1.0 / total)).astype(BF16)
        out = mm_tn(weights, mixed[k, :, v_at])
        before = jnp.where(even, 0.0, hd[k, :, h_at].astype(F32))
        hd[k, :, h_at] = jnp.where(mine_of(even), out, before).astype(BF16)

    own[0].wait()
    own[4].wait()
    qkv_part(0)
    loop(heads, attend)
    fwd(("q", 0), ("o", 0), ("q", 1), ("a", 0), ("o", 1), ("q", 2), ("b", 0), ("a", 1), ("q", 3))()
    loop(parts - 1, lambda k: qkv_part(k + 1))
    loop(
        heads * (parts - 1),
        lambda i: attend(i + heads),
        {
            1: fwd(("o", 2), ("c", 0)),
            2: fwd(("b", 1)),
            3: fwd(("a", 2)),
            4: fwd(("d", 0), ("o", 3)),
            5: fwd(("c", 1)),
            7: fwd(("b", 2), ("a", 3)),
            8: fwd(("d", 1)),
        },
    )
    for made in own[1:4]:
        made.wait()

    def project(n):
        at = pl.ds(pl.multiple_of(n * 256, 256), 256)
        total = tokens[:, at].astype(F32) + vecs[2:3, at]
        for k in range(parts):
            total += mm(hd[k], f_out[k, :, :, :, :, at].reshape(-1, 256))
        resid[:, at] = total

    loop(width // 256, project)

    def norm_two(i):
        r = rows_of(i)
        hat, _ = normalize(resid[r, :])
        normed2[r, :] = (hat * gain(3) + gain(4)).astype(BF16)

    loop(chunks, norm_two)
    hid = f_fc1.shape[5]
    tiles = hid // 256

    def fc1_tile(i):
        k, n = i // tiles, i % tiles
        at = pl.ds(pl.multiple_of(n * 256, 256), 256)
        tile[...] = mm(normed2[...], f_fc1[k, :, :, :, :, at].reshape(width, 256)) + biases[
            k, 1:2, at
        ].astype(F32)

        def gelu(j):
            r = rows_of(j)
            v = tile[r, :]
            cdf = 0.5 * (1.0 + lax.erf(v * (1.0 / math.sqrt(2.0))))
            pdf = jnp.exp(-0.5 * v * v) * (1.0 / math.sqrt(2.0 * math.pi))
            active[k, r, at] = (v * cdf).astype(BF16)
            slope[k, r, at] = (cdf + v * pdf).astype(BF16)

        loop(chunks, gelu)

    loop(tiles, fc1_tile)
    fwd(("c", 2), ("b", 3))()
    loop(
        tiles * (parts - 1),
        lambda i: fc1_tile(i + tiles),
        {2: fwd(("d", 2)), 4: fwd(("c", 3))},
    )

    def grad_branch(i):
        r = rows_of(i)
        g_low[r, :] = (cot[r, :].astype(F32) * cols[r, 1:2]).astype(BF16)

    loop(chunks, grad_branch)
    ones = jnp.ones((8, SEQ), BF16)

    def turn(source):
        def body(n):
            at = pl.ds(pl.multiple_of(n * 256, 256), 256)
            turned[at, :] = source[:, at].astype(F32).T.astype(BF16)

        loop(width // 256, body)

    def weight_grad(target, source, columns, parts_here=parts):
        def body(k):
            for at in range(0, columns, 256):
                size = min(256, columns - at)
                out = mm(turned[...], source[k, :, pl.ds(at, size)])
                target[k, :, :, :, :, pl.ds(at, size)] = out.astype(BF16).reshape(
                    2, 2, 2, width // FAN, size
                )

        return body

    turn(g_low)
    small[1:2, :] = mm(ones, g_low[...])[0:1]
    loop(parts, weight_grad(g_fc2, active, hid))
    red(("A", 0), ("B", 0))()
    fwd(("d", 3))()
    for plan in plans.values():
        for copies in plan:
            left(copies)

    def finish(n):
        at = pl.ds(pl.multiple_of(n * 256, 256), 256)
        total = resid[:, at] + vecs[5:6, at]
        for k in range(parts):
            total += mm(active[k], f_fc2[k, :, :, :, :, at].reshape(hid, 256))
        out = total.astype(BF16)
        ref["output"][:, at] = out
        values = out.astype(F32)
        picked = values * cols[:, 2:3]
        small[4:5, at] = jnp.sum(picked, axis=0, keepdims=True)
        small[5:6, at] = jnp.sum(picked * values, axis=0, keepdims=True)

    loop(width // 256, finish, {2: red(("A", 1))})
    red(("B", 1))()
    small[6:7, :] = jnp.broadcast_to(jnp.sum(cols[:, 2:3], axis=0, keepdims=True), (1, width))
    side = hid // 2

    def hidden_back(i):
        k, s = i // 2, i % 2
        at = pl.ds(pl.multiple_of(s * side, 128), side)
        back = mm_nt(g_low[...], f_fc2[k, s].reshape(side, width))
        back = (back * slope[k, :, at].astype(F32)).astype(BF16)
        slope[k, :, at] = back
        row = pl.ds(8 + (here.t + k) % parts, 1)
        small[row, at] = mm(ones, back)[0:1]

    loop(2 * parts, hidden_back, {6: red(("A", 2))})
    turn(normed2)
    loop(parts, weight_grad(g_fc1, slope, hid))
    red(("C", 0), ("D", 0), ("B", 2))()

    def normed2_back(s):
        at = pl.ds(pl.multiple_of(s * side, 128), side)
        total = mm_nt(slope[0], f_fc1[0, s].reshape(side, hid))
        for k in range(1, parts):
            total += mm_nt(slope[k], f_fc1[k, s].reshape(side, hid))
        acc[:, at] = total

    loop(2, normed2_back, {1: red(("C", 1))})
    red(("D", 1), ("A", 3))()

    def norm_two_back(i):
        r = rows_of(i)
        grad = acc[r, :]
        hat, scale = normalize(resid[r, :])
        back = cot[r, :].astype(F32) * cols[r, 1:2] + normalize_back(hat, scale, gain(3), grad)
        acc[r, :] = back
        g_low[r, :] = back.astype(BF16)
        small[2:3, :] += jnp.sum(grad * hat, axis=0, keepdims=True)
        small[3:4, :] += jnp.sum(grad, axis=0, keepdims=True)
        small[0:1, :] += jnp.sum(back, axis=0, keepdims=True)

    loop(chunks, norm_two_back)
    turn(g_low)
    v_wide = hd.shape[2]
    loop(parts, weight_grad(g_out, hd, v_wide))
    red(("O", 0), ("B", 3))()
    early_round(0)

    def heads_back(k):
        g_heads[k] = mm_nt(g_low[...], f_out[k].reshape(v_wide, width)).astype(BF16)

    loop(parts, heads_back)

    def attend_back(i):
        k, at, v_at, h_at, even = head_place(i)
        mine = mine_of(even)
        scores, kq = scores_of(k, at)
        weights = jnp.exp(scores - lse[i, 0:1, :])
        grad = g_heads[k, :, h_at]
        own_grad = jnp.where(mine, grad.astype(F32), 0.0).astype(BF16)
        g_value = mm(weights.astype(BF16), grad)
        g_weights = mm_nt(mixed[k, :, v_at], own_grad)
        inner = jnp.sum(g_weights * weights, axis=0, keepdims=True)
        g_scores = (weights * (g_weights - inner)).astype(BF16)
        g_q = mm_tn(g_scores, kq)
        g_k = mm(g_scores, kq)
        both = jnp.where(low_half, g_q, g_k) * (1.0 / math.sqrt(HD))
        g_mixed[k, :, at] = both.astype(BF16)
        before = jnp.where(even, 0.0, g_mixed[k, :, v_at].astype(F32))
        g_mixed[k, :, v_at] = jnp.where(mine, g_value, before).astype(BF16)

    turn(normed)

    def qkv_grad(k):
        def run():
            weight_grad(g_qkv, g_mixed, wide)(k)
            units[k].step(0)
            row = pl.ds(2 + (here.t + k) % parts, 1)
            late[row, pl.ds(0, wide)] = mm(ones, g_mixed[k, :, pl.ds(0, wide)])[0:1]

        return run

    hooks = {}

    def hook(at, *runs):
        hooks.setdefault(at, []).extend(runs)

    for k in range(1, parts):
        hook(heads * k, qkv_grad(k - 1))
    hook(1, red(("C", 2)))
    hook(2, red(("O", 1)))
    hook(5, red(("D", 2)))
    hook(7, red((0, 1)))
    hook(8, red(("A", 4), ("C", 3)))
    hook(9, red((1, 1)))
    hook(10, red(("O", 2)))
    hook(11, red(("D", 3), (0, 2)))
    for r in range(1, len(trips) + 1):
        hook(min(2 * r, heads * parts - 1), partial(early_round, r))

    def joined(runs):
        def run():
            for one in runs:
                one()

        return run

    loop(heads * parts, attend_back, {at: joined(runs) for at, runs in hooks.items()})
    qkv_grad(parts - 1)()
    for k in range(2, parts - 1):
        red((k, 1))()

    def normed_back(s):
        at = pl.ds(pl.multiple_of(s * side, 128), side)
        total = mm_nt(g_mixed[0, :, pl.ds(0, wide)], f_qkv[0, s].reshape(side, wide))
        for k in range(1, parts):
            total += mm_nt(g_mixed[k, :, pl.ds(0, wide)], f_qkv[k, s].reshape(side, wide))
        tile_out = total
        resid[:, at] = tile_out

    loop(2, normed_back, {1: red((parts - 1, 1), (1, 2), ("O", 3))})

    def norm_one_back(i):
        r = rows_of(i)
        grad = resid[r, :]
        hat, scale = normalize(tokens[r, :].astype(F32))
        back = acc[r, :] + normalize_back(hat, scale, gain(0), grad)
        ref["g_tokens"][r, :] = back.astype(BF16)
        late[0:1, :] += jnp.sum(grad * hat, axis=0, keepdims=True)
        late[1:2, :] += jnp.sum(grad, axis=0, keepdims=True)

    loop(chunks, norm_one_back)
    late_round(0)
    for k in range(2, parts):
        red((k, 2))()
    late_round(1)
    for k in range(parts):
        red((k, 3))()
    late_round(2)
    final = sums.at[len(trips)]
    mean = final[4:5, :] / final[6:7, :]
    spread = final[5:6, :] / final[6:7, :] - mean * mean
    spread = lax.rsqrt(spread + 1e-05)

    def features(i):
        r = rows_of(i)
        ref["cls"][r, :] = cols[r, 2:3] * (ref["output"][r, :].astype(F32) - mean) * spread

    loop(chunks, features)
    late_round(3)
    red(("B", 4), ("C", 4), ("D", 4), ("O", 4))()
    total(columns(g_fc2, 0, cut), got_z[0], ref["s_fc2"].at[:, pl.ds(0, cut)])
    total(columns(g_fc2, cut, cut), got_z[1], ref["s_fc2"].at[:, pl.ds(cut, cut)])
    total(columns(g_fc1, 0, cut), got_z[2], ref["s_fc1"].at[:, pl.ds(0, cut)])
    total(columns(g_fc1, cut, cut), got_z[3], ref["s_fc1"].at[:, pl.ds(cut, cut)])
    total(g_out, got_z[4], ref["s_out"])
    for r in range(4, len(late_trips) + 1):
        late_round(r)
    for k in range(parts):
        red((k, 4))()
    total(g_qkv, got_z[UNITS], ref["s_qkv"])
    ref["small"][...] = final[...]
    ref["late"][...] = ref["late_sums"][len(late_trips)]
    left(trips + late_trips)
    for unit in units.values():
        unit.drain()


def layer(tokens, cot, segments, vecs, bias, shards, dp_size, parts, heads):
    shards = [s.reshape(2, 2, 2, s.shape[0] // FAN, s.shape[1]) for s in shards]
    width, hid = tokens.shape[1], shards[2].shape[4]
    wide, v_wide = shards[0].shape[4], FAN * shards[1].shape[3]
    lines, late_lines = -(-(8 + parts) // 8) * 8, -(-(2 + parts) // 8) * 8
    rounds = dp_size.bit_length() - 1 + parts.bit_length() - 1
    copies = 6 * (5 + parts - 1) + parts - 1 + (UNITS + parts) * (5 + parts) + 2 * rounds
    blk = width // FAN
    grads = [(blk, wide), (blk, v_wide), (blk, hid), (blk, hid)]
    whole = [pltpu.VMEM((parts,) + s.shape, BF16) for s in shards]
    scratch = whole + [
        pltpu.VMEM((parts,) + bias.shape, BF16),
        pltpu.VMEM((SEQ, width), BF16),
        pltpu.VMEM((parts, SEQ, wide), BF16),
        pltpu.VMEM((SEQ, SEQ), F32),
        pltpu.VMEM((parts * heads, 8, SEQ), F32),
        pltpu.VMEM((parts, SEQ, v_wide), BF16),
        pltpu.VMEM((SEQ, width), F32),
        pltpu.VMEM((SEQ, width), BF16),
        pltpu.VMEM((parts, SEQ, hid), BF16),
        pltpu.VMEM((parts, SEQ, hid), BF16),
        pltpu.VMEM((width, SEQ), BF16),
        pltpu.VMEM((SEQ, width), F32),
        pltpu.VMEM((SEQ, 256), F32),
        pltpu.VMEM((SEQ, width), BF16),
        pltpu.VMEM((parts, SEQ, v_wide), BF16),
        pltpu.VMEM((parts, 2, 2, 2, blk, hid), BF16),
        pltpu.VMEM((parts, 2, 2, 2, blk, v_wide), BF16),
        pltpu.VMEM((SEQ, 8), F32),
        pltpu.VMEM((rounds + 1, lines, width), F32),
        pltpu.VMEM((rounds, lines, width), F32),
        pltpu.VMEM((rounds + 1, late_lines, width), F32),
        pltpu.VMEM((rounds, late_lines, width), F32),
    ]
    sizes = [(parts, hid // 2)] * 4 + [(parts, v_wide)] + [(1, wide)] * parts
    for many, n in sizes:
        for lead, half in (((many, 2, 2), 1), ((many, 2), 2), ((many,), 2), ((many, 2), 2), ((many,), 2)):
            scratch.append(pltpu.VMEM(lead + (blk // half, n), BF16))
    for _, n in sizes[: UNITS + 1]:
        scratch.append(pltpu.VMEM((parts - 1, blk, n), BF16))
    scratch += [
        pltpu.SemaphoreType.DMA((5,)),
        pltpu.SemaphoreType.DMA((copies,)),
        pltpu.SemaphoreType.DMA((copies,)),
    ]
    shape = jax.ShapeDtypeStruct
    return pl.pallas_call(
        partial(layer_kernel, dp_size, parts, heads),
        out_shape=[shape(tokens.shape, BF16), shape(tokens.shape, BF16)]
        + [shape(g, F32) for g in grads]
        + [shape((lines, width), F32), shape((late_lines, width), F32), shape(tokens.shape, F32)],
        in_specs=[VMEM] * 4 + [ANY] * 5,
        out_specs=[VMEM] * 9,
        scratch_shapes=scratch,
        compiler_params=pltpu.CompilerParams(
            collective_id=0, has_side_effects=True, vmem_limit_bytes=67043328
        ),
    )(tokens, cot, segments, vecs, bias, *shards)


def regroup(columns, heads):
    lead = columns.shape[:-1]
    split = columns.reshape(lead + (heads, 3, HD))
    pairs = split[..., :2, :].reshape(lead + (heads * 2 * HD,))
    values = split[..., 2, :].reshape(lead + (heads * HD,))
    pad = jnp.zeros(lead + (heads % 2 * HD,), columns.dtype)
    return jnp.concatenate([pairs, values, pad], axis=-1)


def ungroup(columns, heads):
    lead = columns.shape[:-1]
    pairs = columns[..., : heads * 2 * HD].reshape(lead + (heads, 2, HD))
    values = columns[..., heads * 2 * HD : heads * 3 * HD].reshape(lead + (heads, 1, HD))
    return jnp.concatenate([pairs, values], axis=-2)


def on_device(dp_size, parts, tokens, segments, cotangent, ln1_gain, ln1_bias, w_qkv, q_bias, v_bias, w_out, out_bias, ln2_gain, ln2_bias, w_fc1, fc1_bias, w_fc2, fc2_bias):
    tensor_index = lax.axis_index("tensor")
    rows, width = tokens.shape
    head_cols = w_out.shape[0]
    heads = head_cols // HD
    hidden_cols = w_fc1.shape[1]
    vecs = jnp.concatenate([ln1_gain, ln1_bias, out_bias, ln2_gain, ln2_bias, fc2_bias, fc2_bias, fc2_bias])
    vecs = vecs.reshape(8, width).astype(F32)
    out_rows = -(-head_cols // 128) * 128
    out_padded = jnp.pad(w_out, ((0, out_rows - head_cols), (0, 0)))
    qkv = regroup(w_qkv, heads)
    line = max(qkv.shape[1], hidden_cols)
    none = jnp.zeros((16 * line,), BF16)
    pieces = []
    for h in range(heads):
        pieces += [q_bias[h * HD : (h + 1) * HD], none[:HD]]
    pieces += [v_bias, none[: line - 3 * head_cols], fc1_bias, none[: 15 * line - hidden_cols]]
    bias = jnp.concatenate(pieces).reshape(16, line)

    output, grad_tokens, sum_qkv, sum_out, sum_fc1, sum_fc2, small, late, cls_features = layer(
        tokens, cotangent, segments.reshape(-1, SEQ), vecs, bias, [qkv, out_padded, w_fc1, w_fc2], dp_size, parts, heads
    )
    sum_qkv = ungroup(sum_qkv, heads).reshape(sum_qkv.shape[0], -1)
    sum_out = sum_out[:, :head_cols]
    low = dp_size // FAN

    def finish(array):
        if low == 1:
            return array
        groups = [[i * low + j for j in range(low)] for i in range(FAN)]
        return lax.psum_scatter(array, "dp", scatter_dimension=0, axis_index_groups=groups, tiled=True)

    sum_qkv, sum_out, sum_fc1, sum_fc2 = (finish(a) for a in (sum_qkv, sum_out, sum_fc1, sum_fc2))
    mixed_sums = ungroup(late[2 : 2 + parts, : qkv.shape[1]], heads)
    return (
        output,
        grad_tokens,
        cls_features,
        sum_qkv,
        mixed_sums[:, :, 0].reshape(-1),
        mixed_sums[:, :, 2].reshape(-1),
        sum_out.T,
        small[0],
        sum_fc1,
        small[8 : 8 + parts, :hidden_cols].reshape(-1),
        sum_fc2.T,
        small[1],
        late[0],
        late[1],
        small[2],
        small[3],
    )


def solution(mesh):
    dp_size, parts = mesh.shape["dp"], mesh.shape["tensor"]
    row, whole, cols, out_cols = P(("dp", "tensor"), None), P(), P(None, "tensor"), P("tensor")
    down = P("tensor", None)
    in_specs = (row, P("dp"), row, whole, whole, cols, out_cols, out_cols, down, whole, whole, whole, cols, out_cols, down, whole)
    spread, turned = P("dp", "tensor"), P("tensor", "dp")
    out_specs = (row, row, row, spread, whole, whole, turned, whole, spread, whole, turned, whole, whole, whole, whole, whole)
    return jax.shard_map(partial(on_device, dp_size, parts), mesh=mesh, in_specs=in_specs, out_specs=out_specs, check_vma=False)
```

profile of v0, /device:TPU:0, one launch (start us, length us, event | category | flops | bytes accessed | tf_op | source)
XLA Modules:
  0.0 214.2 jit_solution(16302997178899619775)
XLA Ops:
  0.6 0.0 copy-start.4
  0.7 0.0 copy-start.1
  0.7 0.9 fusion
  1.5 0.1 pad.9.clone
  1.6 1.3 reshape.75.refs_2_
  2.9 0.8 dynamic-update-slice
  3.8 0.8 dynamic-update-slice.1
  4.6 0.9 dynamic-update-slice.2
  5.5 0.9 dynamic-update-slice.3
  6.3 0.9 dynamic-update-slice.4
  7.2 0.8 dynamic-update-slice.5
  8.0 0.9 dynamic-update-slice.6
  8.9 0.8 dynamic-update-slice.7
  9.7 0.6 reshape.86.refs_3_
  10.4 1.4 concatenate.18
  11.8 0.7 reshape.76.refs_4_
  12.4 1.0 slice_bitcast_fusion
  13.4 0.4 concatenate.20
  13.9 0.5 copy.38
  14.4 0.0 copy-done.4
  14.4 0.8 pad.4
  15.1 0.0 copy-done.1
  15.2 0.8 concatenate.19
  16.0 0.7 copy.37
  16.7 1.1 maximum_maximum_fusion.refs_5_
  17.8 181.5 %shard_map.279 = (bf16[512,768]{1,0:T(8,128)(2,1)}, bf16[512,768]{1,0:T(8,128)(2,1)}, f32[96,640]{1,0:T(8,128)}, f32[96,256]{1,0:T(8,128)}, f32[96,768]{1,0:T(8,...) custom-call(bf16[512,768]{1,0:T(8,128)(2,1)} %refs_0_.1, ...), custom_call_target="tpu_custom_call" | custom-call | tf_op jit(solution)/shard_map/pallas_call | solution.py:754
  199.3 0.0 copy-start.3
  199.3 0.8 slice.74
  200.1 0.7 reshape_squeeze_reshape.3
  200.8 0.7 slice.72
  201.5 1.6 slice_reduce_fusion.1
  203.1 0.7 slice.77
  203.8 0.6 reshape.85
  204.5 0.1 reshape.84
  204.6 0.7 reshape_squeeze.4
  205.2 0.9 slice_bitcast_fusion.1
  206.1 0.7 copy.43
  206.9 0.9 slice.71
  207.8 0.9 slice.70
  208.7 0.1 copy.40
  208.8 0.0 copy-start.2
  208.8 0.1 copy.39
  209.0 0.9 copy.42
  209.8 0.0 copy-done.3
  209.8 0.0 copy-start
  209.8 0.9 copy.58
  210.7 0.0 copy-done.2
  210.7 0.9 copy.59
  211.6 0.0 copy-done
  211.6 0.0 copy-start.6
  211.6 0.0 copy-start.5
  211.6 1.1 copy.60
  212.7 0.0 copy-done.6
  212.7 0.7 copy.61
  213.5 0.0 copy-done.5
  213.5 0.7 copy.62
  (7 shorter events, 0.1 us)
Async XLA Ops:
  0.6 13.7 %copy-start.4 = (bf16[192,768]{1,0:T(8,128)(2,1)S(1)}, bf16[192,768]{1,0:T(8,128)(2,1)}, u32[]{:S(2)}) copy-start(bf16[192,768]{1,0:T(8,128)(2,1)} %param.24) | copy-start | bytes 884740
  0.7 14.5 %copy-start.1 = (bf16[768,576]{0,1:T(8,128)(2,1)S(1)}, bf16[768,576]{0,1:T(8,128)(2,1)}, u32[]{:S(2)}) copy-start(bf16[768,576]{0,1:T(8,128)(2,1)} %param.21) | copy-start | bytes 2654212
  199.3 10.5 %copy-start.3 = (bf16[512,768]{1,0:T(8,128)(2,1)S(1)}, bf16[512,768]{1,0:T(8,128)(2,1)}, u32[]{:S(2)}) copy-start(bf16[512,768]{1,0:T(8,128)(2,1)} %get-tuple-element.93) | copy-start | bytes 2359300
  208.8 1.9 copy-start.2
  209.8 1.8 copy-start
  211.6 1.1 copy-start.6
  211.6 1.9 copy-start.5
where the time goes:
time: 215 us; the launch traced here: 214 us
  Pallas kernels  181 us (84%)
  local copies, waits for them, and re-layouts  30.8 us (14%)
    pallas_call x1, Pallas kernels, layer(): pl.pallas_call(partial(layer_kernel, dp_size, parts, heads), out_shape=[s...  181 us
    unnamed x29, local copies, waits for them, and re-layouts  12.9 us

commit v1 on v0

--- a/solution.py
+++ b/solution.py
@@ -3,6 +3,7 @@
 
 import jax
 import jax.numpy as jnp
+import numpy as np
 from jax import lax
 from jax.experimental import pallas as pl
 from jax.experimental.pallas import tpu as pltpu
@@ -132,7 +133,62 @@
     second = [link.copy(a, a, here.flip("y")), link.copy(b, b, here.flip("x"))]
     a = whole.at[away, :, :, c]
     third = [link.copy(a, a, here.flip("c"))]
-    return [along, first, second, third]
+    relay = None
+    if parts == 4:
+        over = whole.at[2, y, x, c]
+        relay = [
+            link.copy(over, whole.at[1, y, x, c], here.shift(1)),
+            link.copy(over, whole.at[3, y, x, c], here.shift(3)),
+        ]
+    return Gather(here, along, relay, [first, second, third])
+
+
+class Gather:
+    def __init__(self, here, along, relay, later):
+        self.t, self.along, self.relay, self.later = here.t, along, relay, later
+
+    def guarded(self, what, does):
+        if self.relay is None:
+            for made in self.along:
+                does(made)
+            return
+        up, across, down = self.along[:3]
+        ends = (self.t < 3, self.t > 0) if what == "out" else (self.t > 0, self.t < 3)
+        pl.when(ends[0])(lambda: does(up))
+        does(across)
+        pl.when(ends[1])(lambda: does(down))
+        for made in self.along[3:]:
+            does(made)
+
+    def relayed(self, what, does):
+        up, down = self.relay
+        at = (2, 1) if what == "out" else (3, 0)
+        pl.when(self.t == at[0])(lambda: does(up))
+        pl.when(self.t == at[1])(lambda: does(down))
+
+    def begin(self):
+        self.guarded("out", lambda made: made.start())
+
+    def step(self, s):
+        if s == "z":
+            self.guarded("in", lambda made: made.wait_recv())
+            if self.relay is not None:
+                self.relayed("out", lambda made: made.start())
+            return
+        if s == 0:
+            if self.relay is not None:
+                self.relayed("in", lambda made: made.wait_recv())
+        else:
+            arrive(self.later[s - 1])
+        if s < 3:
+            start(self.later[s])
+
+    def drain(self):
+        self.guarded("out", lambda made: made.wait_send())
+        if self.relay is not None:
+            self.relayed("out", lambda made: made.wait_send())
+        for copies in self.later:
+            left(copies)
 
 
 class Reduction:
@@ -220,7 +276,6 @@
     "s_fc1",
     "s_fc2",
     "small",
-    "late",
     "cls",
 )
 SCRATCH = (
@@ -240,7 +295,6 @@
     "slope",
     "turned",
     "acc",
-    "tile",
     "g_low",
     "g_heads",
     "g_fc2",
@@ -248,8 +302,7 @@
     "cols",
     "sums",
     "got_small",
-    "late_sums",
-    "got_late",
+    "all_sums",
 )
 
 
@@ -267,14 +320,15 @@
     biases, normed, mixed, mask = ref["biases"], ref["normed"], ref["mixed"], ref["mask"]
     lse, hd, resid, normed2 = ref["lse"], ref["heads"], ref["resid"], ref["normed2"]
     active, slope, turned, acc = ref["active"], ref["slope"], ref["turned"], ref["acc"]
-    tile, g_low, g_heads, sums = ref["tile"], ref["g_low"], ref["g_heads"], ref["sums"]
+    tile = acc.at[:, pl.ds(0, 256)]
+    g_low, g_heads, sums = ref["g_low"], ref["g_heads"], ref["sums"]
     g_fc2, g_out = ref["g_fc2"], ref["g_out"]
     g_mixed = active
     wide = f_qkv.shape[5]
     g_qkv = f_fc1.at[:, :, :, :, :, pl.ds(0, wide)]
     g_fc1 = f_fc2
     width = tokens.shape[1]
-    small, late = sums.at[0], ref["late_sums"].at[0]
+    small = sums.at[0]
     here = Place(dp_size, parts)
     qk_wide = heads * 128
     strides = [1 << b for b in range(dp_size.bit_length() - 1)]
@@ -298,11 +352,11 @@
         plans[name] = gather_unit(
             here, link, columns(shards[i], first, cut), columns(wholes[i], first, cut)
         )
-    plans["q"][0] += [
+    plans["q"].along += [
         link.copy(ref["bias"], biases.at[parts - k], here.shift(k)) for k in range(1, parts)
     ]
-    for plan in plans.values():
-        start(plan[0])
+    for name in "qoa":
+        plans[name].begin()
     units = {}
     for i, (name, grad) in enumerate(
         (
@@ -320,9 +374,10 @@
     def fwd(*steps):
         def run():
             for name, s in steps:
-                arrive(plans[name][s])
-                if s < 3:
-                    start(plans[name][s + 1])
+                if s == "go":
+                    plans[name].begin()
+                else:
+                    plans[name].step(s)
 
         return run
 
@@ -333,37 +388,34 @@
 
         return run
 
-    def total(grad, got_last, out):
+    def total(grad, got_last, out=None):
         value = grad[0, here.y, here.x, here.c].astype(F32)
         for k in range(parts - 1):
             value += got_last[k].astype(F32)
+        if out is None:
+            return value
         out[...] = value
 
-    tensor_bits = [
-        (here.d, here.t + (1 << b) * (1 - 2 * ((here.t // (1 << b)) % 2)))
-        for b in range(parts.bit_length() - 1)
+    trips = [
+        link.copy(sums.at[r], ref["got_small"].at[r], partner) for r, partner in enumerate(bits)
     ]
-
-    def butterfly(slots, got_slots):
-        trips = [
-            link.copy(slots.at[r], got_slots.at[r], partner)
-            for r, partner in enumerate(bits + tensor_bits)
-        ]
-
-        def run(r):
-            if r > 0:
-                arrive([trips[r - 1]])
-                slots[r] = slots[r - 1] + got_slots[r - 1]
-            if r < len(trips):
-                start([trips[r]])
-
-        return trips, run
-
-    trips, early_round = butterfly(sums, ref["got_small"])
-    late_trips, late_round = butterfly(ref["late_sums"], ref["got_late"])
+    all_sums = ref["all_sums"]
+    spread_out = [
+        link.copy(sums.at[len(bits)], all_sums.at[here.t], here.shift(k)) for k in range(1, parts)
+    ]
+
+    def small_round(r):
+        if r > 0:
+            arrive([trips[r - 1]])
+            sums[r] = sums[r - 1] + ref["got_small"][r - 1]
+        if r < len(trips):
+            start([trips[r]])
+        else:
+            start(spread_out)
+            all_sums[here.t] = sums[r]
 
     def gain(i):
-        return vecs[pl.ds(i, 1), :]
+        return vecs[pl.ds(i, 1), :].astype(F32)
 
     chunks = SEQ // ROWS
 
@@ -371,8 +423,9 @@
         return pl.ds(pl.multiple_of(i * ROWS, ROWS), ROWS)
 
     small[...] = jnp.zeros_like(small)
-    late[...] = jnp.zeros_like(late)
-    labels = segments[pl.ds(here.t, 1), :]
+    labels = jnp.concatenate(
+        [segments[pl.ds(here.t * (SEQ // 128) + i, 1), :] for i in range(SEQ // 128)], axis=1
+    )
     spot = lax.broadcasted_iota(jnp.int32, (1, SEQ), 1)
     earlier = pltpu.roll(labels, 1, 1)
     begins = (labels >= 0) & ((spot == 0) | (labels != earlier))
@@ -391,11 +444,21 @@
 
     low_half = lax.broadcasted_iota(jnp.int32, (SEQ, 128), 1) < 64
 
+    head_cols = heads * HD
+    pick = active.at[0, pl.ds(0, 2 * head_cols), pl.ds(0, wide)]
+    taken = lax.broadcasted_iota(jnp.int32, (2 * head_cols, wide), 0)
+    slot = lax.broadcasted_iota(jnp.int32, (2 * head_cols, wide), 1)
+    lane = slot % 128
+    of_q = (slot < qk_wide) & (lane < HD) & (taken == (slot // 128) * HD + lane)
+    of_v = (slot >= qk_wide) & (taken == head_cols + slot - qk_wide)
+    pick[...] = jnp.where(of_q | of_v, 1.0, 0.0).astype(BF16)
+
     def qkv_part(k):
+        offset = mm(biases[k, :, pl.ds(0, 2 * head_cols)].astype(BF16), pick[...])[6:7]
         for at in range(0, wide, 256):
             size = min(256, wide - at)
             w = f_qkv[k, :, :, :, :, pl.ds(at, size)].reshape(width, size)
-            out = mm(normed[...], w) + biases[k, 0:1, pl.ds(at, size)].astype(F32)
+            out = mm(normed[...], w) + offset[:, at : at + size]
             mixed[k, :, pl.ds(at, size)] = out.astype(BF16)
 
     def head_place(i):
@@ -430,20 +493,23 @@
     own[0].wait()
     own[4].wait()
     qkv_part(0)
-    loop(heads, attend)
-    fwd(("q", 0), ("o", 0), ("q", 1), ("a", 0), ("o", 1), ("q", 2), ("b", 0), ("a", 1), ("q", 3))()
+    loop(heads, attend, {1: fwd(("q", "z"))})
+    fwd(("o", "z"), ("b", "go"), ("q", 0), ("o", 0))()
+    fwd(("a", "z"), ("c", "go"), ("q", 1), ("a", 0), ("o", 1), ("b", "z"), ("d", "go"), ("q", 2))()
+    fwd(("b", 0), ("a", 1), ("c", "z"), ("q", 3))()
     loop(parts - 1, lambda k: qkv_part(k + 1))
     loop(
         heads * (parts - 1),
         lambda i: attend(i + heads),
         {
-            1: fwd(("o", 2), ("c", 0)),
-            2: fwd(("b", 1)),
+            1: fwd(("o", 2), ("c", 0), ("d", "z")),
+            2: fwd(("b", 1), ("d", 0)),
             3: fwd(("a", 2)),
-            4: fwd(("d", 0), ("o", 3)),
+            4: fwd(("o", 3)),
             5: fwd(("c", 1)),
-            7: fwd(("b", 2), ("a", 3)),
-            8: fwd(("d", 1)),
+            6: fwd(("b", 2), ("a", 3)),
+            7: fwd(("d", 1)),
+            8: fwd(("c", 2)),
         },
     )
     for made in own[1:4]:
@@ -451,7 +517,7 @@
 
     def project(n):
         at = pl.ds(pl.multiple_of(n * 256, 256), 256)
-        total = tokens[:, at].astype(F32) + vecs[2:3, at]
+        total = tokens[:, at].astype(F32) + vecs[2:3, at].astype(F32)
         for k in range(parts):
             total += mm(hd[k], f_out[k, :, :, :, :, at].reshape(-1, 256))
         resid[:, at] = total
@@ -471,7 +537,7 @@
         k, n = i // tiles, i % tiles
         at = pl.ds(pl.multiple_of(n * 256, 256), 256)
         tile[...] = mm(normed2[...], f_fc1[k, :, :, :, :, at].reshape(width, 256)) + biases[
-            k, 1:2, at
+            k, 7:8, at
         ].astype(F32)
 
         def gelu(j):
@@ -485,7 +551,7 @@
         loop(chunks, gelu)
 
     loop(tiles, fc1_tile)
-    fwd(("c", 2), ("b", 3))()
+    fwd(("b", 3))()
     loop(
         tiles * (parts - 1),
         lambda i: fc1_tile(i + tiles),
@@ -523,12 +589,11 @@
     red(("A", 0), ("B", 0))()
     fwd(("d", 3))()
     for plan in plans.values():
-        for copies in plan:
-            left(copies)
+        plan.drain()
 
     def finish(n):
         at = pl.ds(pl.multiple_of(n * 256, 256), 256)
-        total = resid[:, at] + vecs[5:6, at]
+        total = resid[:, at] + vecs[5:6, at].astype(F32)
         for k in range(parts):
             total += mm(active[k], f_fc2[k, :, :, :, :, at].reshape(hid, 256))
         out = total.astype(BF16)
@@ -549,7 +614,7 @@
         back = mm_nt(g_low[...], f_fc2[k, s].reshape(side, width))
         back = (back * slope[k, :, at].astype(F32)).astype(BF16)
         slope[k, :, at] = back
-        row = pl.ds(8 + (here.t + k) % parts, 1)
+        row = pl.ds(10 + (here.t + k) % parts, 1)
         small[row, at] = mm(ones, back)[0:1]
 
     loop(2 * parts, hidden_back, {6: red(("A", 2))})
@@ -583,7 +648,6 @@
     v_wide = hd.shape[2]
     loop(parts, weight_grad(g_out, hd, v_wide))
     red(("O", 0), ("B", 3))()
-    early_round(0)
 
     def heads_back(k):
         g_heads[k] = mm_nt(g_low[...], f_out[k].reshape(v_wide, width)).astype(BF16)
@@ -614,8 +678,8 @@
         def run():
             weight_grad(g_qkv, g_mixed, wide)(k)
             units[k].step(0)
-            row = pl.ds(2 + (here.t + k) % parts, 1)
-            late[row, pl.ds(0, wide)] = mm(ones, g_mixed[k, :, pl.ds(0, wide)])[0:1]
+            row = pl.ds(10 + parts + (here.t + k) % parts, 1)
+            small[row, pl.ds(0, wide)] = mm(ones, g_mixed[k, :, pl.ds(0, wide)])[0:1]
 
         return run
 
@@ -634,8 +698,6 @@
     hook(9, red((1, 1)))
     hook(10, red(("O", 2)))
     hook(11, red(("D", 3), (0, 2)))
-    for r in range(1, len(trips) + 1):
-        hook(min(2 * r, heads * parts - 1), partial(early_round, r))
 
     def joined(runs):
         def run():
@@ -665,18 +727,57 @@
         hat, scale = normalize(tokens[r, :].astype(F32))
         back = acc[r, :] + normalize_back(hat, scale, gain(0), grad)
         ref["g_tokens"][r, :] = back.astype(BF16)
-        late[0:1, :] += jnp.sum(grad * hat, axis=0, keepdims=True)
-        late[1:2, :] += jnp.sum(grad, axis=0, keepdims=True)
+        small[8:9, :] += jnp.sum(grad * hat, axis=0, keepdims=True)
+        small[9:10, :] += jnp.sum(grad, axis=0, keepdims=True)
 
     loop(chunks, norm_one_back)
-    late_round(0)
+    small_round(0)
     for k in range(2, parts):
         red((k, 2))()
-    late_round(1)
+    red(("B", 4), ("C", 4), ("D", 4), ("O", 4))()
+    small_round(1)
+    total(columns(g_fc1, 0, cut), got_z[2], ref["s_fc1"].at[:, pl.ds(0, cut)])
+    total(columns(g_fc1, cut, cut), got_z[3], ref["s_fc1"].at[:, pl.ds(cut, cut)])
     for k in range(parts):
         red((k, 3))()
-    late_round(2)
-    final = sums.at[len(trips)]
+    small_round(2)
+    total(g_out, got_z[4], ref["s_out"])
+    for r in range(3, len(trips) + 1):
+        small_round(r)
+    for i, first in enumerate((0, cut)):
+        total(columns(g_fc2, first, cut), got_z[i], ref["s_fc2"].at[:, pl.ds(first, cut)])
+    for k in range(parts):
+        red((k, 4))()
+    triple = 3 * HD
+    source = lax.broadcasted_iota(jnp.int32, (wide, heads * triple), 0)
+    target = lax.broadcasted_iota(jnp.int32, (wide, heads * triple), 1)
+    head, lane = target // triple, target % triple
+    wanted = jnp.where(lane < 2 * HD, head * 2 * HD + lane, qk_wide + head * HD + lane - 2 * HD)
+    unpick = jnp.where(source == wanted, 1.0, 0.0)
+    ref["s_qkv"][...] = lax.dot_general(
+        total(g_qkv, got_z[UNITS]),
+        unpick,
+        (((1,), (0,)), ((), ())),
+        precision=lax.Precision.HIGHEST,
+        preferred_element_type=F32,
+    )
+    arrive(spread_out)
+    final = all_sums[0]
+    for t in range(1, parts):
+        final += all_sums[t]
+    ref["small"][...] = final
+    source = lax.broadcasted_iota(jnp.int32, (wide, 2 * head_cols), 0)
+    target = lax.broadcasted_iota(jnp.int32, (wide, 2 * head_cols), 1)
+    wanted = jnp.where(
+        target < head_cols, (target // HD) * 2 * HD + target % HD, qk_wide + target - head_cols
+    )
+    ref["small"][pl.ds(10 + parts, parts), pl.ds(0, 2 * head_cols)] = lax.dot_general(
+        final[:, :wide],
+        jnp.where(source == wanted, 1.0, 0.0),
+        (((1,), (0,)), ((), ())),
+        precision=lax.Precision.HIGHEST,
+        preferred_element_type=F32,
+    )[10 + parts : 10 + 2 * parts]
     mean = final[4:5, :] / final[6:7, :]
     spread = final[5:6, :] / final[6:7, :] - mean * mean
     spread = lax.rsqrt(spread + 1e-05)
@@ -686,37 +787,23 @@
         ref["cls"][r, :] = cols[r, 2:3] * (ref["output"][r, :].astype(F32) - mean) * spread
 
     loop(chunks, features)
-    late_round(3)
-    red(("B", 4), ("C", 4), ("D", 4), ("O", 4))()
-    total(columns(g_fc2, 0, cut), got_z[0], ref["s_fc2"].at[:, pl.ds(0, cut)])
-    total(columns(g_fc2, cut, cut), got_z[1], ref["s_fc2"].at[:, pl.ds(cut, cut)])
-    total(columns(g_fc1, 0, cut), got_z[2], ref["s_fc1"].at[:, pl.ds(0, cut)])
-    total(columns(g_fc1, cut, cut), got_z[3], ref["s_fc1"].at[:, pl.ds(cut, cut)])
-    total(g_out, got_z[4], ref["s_out"])
-    for r in range(4, len(late_trips) + 1):
-        late_round(r)
-    for k in range(parts):
-        red((k, 4))()
-    total(g_qkv, got_z[UNITS], ref["s_qkv"])
-    ref["small"][...] = final[...]
-    ref["late"][...] = ref["late_sums"][len(late_trips)]
-    left(trips + late_trips)
+    left(trips + spread_out)
     for unit in units.values():
         unit.drain()
 
 
-def layer(tokens, cot, segments, vecs, bias, shards, dp_size, parts, heads):
+def layer(tokens, cot, segments, bias, shards, dp_size, parts, heads):
     shards = [s.reshape(2, 2, 2, s.shape[0] // FAN, s.shape[1]) for s in shards]
     width, hid = tokens.shape[1], shards[2].shape[4]
     wide, v_wide = shards[0].shape[4], FAN * shards[1].shape[3]
-    lines, late_lines = -(-(8 + parts) // 8) * 8, -(-(2 + parts) // 8) * 8
-    rounds = dp_size.bit_length() - 1 + parts.bit_length() - 1
-    copies = 6 * (5 + parts - 1) + parts - 1 + (UNITS + parts) * (5 + parts) + 2 * rounds
+    lines = -(-(10 + 2 * parts) // 8) * 8
+    rounds = dp_size.bit_length() - 1
+    copies = 6 * (5 + parts + 1) + parts - 1 + (UNITS + parts) * (5 + parts) + rounds + parts
     blk = width // FAN
     grads = [(blk, wide), (blk, v_wide), (blk, hid), (blk, hid)]
     whole = [pltpu.VMEM((parts,) + s.shape, BF16) for s in shards]
     scratch = whole + [
-        pltpu.VMEM((parts,) + bias.shape, BF16),
+        pltpu.VMEM((parts,) + bias.shape, F32),
         pltpu.VMEM((SEQ, width), BF16),
         pltpu.VMEM((parts, SEQ, wide), BF16),
         pltpu.VMEM((SEQ, SEQ), F32),
@@ -728,7 +815,6 @@
         pltpu.VMEM((parts, SEQ, hid), BF16),
         pltpu.VMEM((width, SEQ), BF16),
         pltpu.VMEM((SEQ, width), F32),
-        pltpu.VMEM((SEQ, 256), F32),
         pltpu.VMEM((SEQ, width), BF16),
         pltpu.VMEM((parts, SEQ, v_wide), BF16),
         pltpu.VMEM((parts, 2, 2, 2, blk, hid), BF16),
@@ -736,8 +822,7 @@
         pltpu.VMEM((SEQ, 8), F32),
         pltpu.VMEM((rounds + 1, lines, width), F32),
         pltpu.VMEM((rounds, lines, width), F32),
-        pltpu.VMEM((rounds + 1, late_lines, width), F32),
-        pltpu.VMEM((rounds, late_lines, width), F32),
+        pltpu.VMEM((parts, lines, width), F32),
     ]
     sizes = [(parts, hid // 2)] * 4 + [(parts, v_wide)] + [(1, wide)] * parts
     for many, n in sizes:
@@ -754,31 +839,24 @@
     return pl.pallas_call(
         partial(layer_kernel, dp_size, parts, heads),
         out_shape=[shape(tokens.shape, BF16), shape(tokens.shape, BF16)]
-        + [shape(g, F32) for g in grads]
-        + [shape((lines, width), F32), shape((late_lines, width), F32), shape(tokens.shape, F32)],
+        + [shape((blk, heads * 3 * HD), F32), shape((blk, v_wide), F32), shape((blk, hid), F32), shape((blk, hid), F32)]
+        + [shape((lines, width), F32), shape(tokens.shape, F32)],
         in_specs=[VMEM] * 4 + [ANY] * 5,
-        out_specs=[VMEM] * 9,
+        out_specs=[VMEM] * 8,
         scratch_shapes=scratch,
         compiler_params=pltpu.CompilerParams(
             collective_id=0, has_side_effects=True, vmem_limit_bytes=67043328
         ),
-    )(tokens, cot, segments, vecs, bias, *shards)
+    )(tokens, cot, segments, bias, bias, *shards)
 
 
 def regroup(columns, heads):
-    lead = columns.shape[:-1]
-    split = columns.reshape(lead + (heads, 3, HD))
-    pairs = split[..., :2, :].reshape(lead + (heads * 2 * HD,))
-    values = split[..., 2, :].reshape(lead + (heads * HD,))
-    pad = jnp.zeros(lead + (heads % 2 * HD,), columns.dtype)
-    return jnp.concatenate([pairs, values, pad], axis=-1)
-
-
-def ungroup(columns, heads):
-    lead = columns.shape[:-1]
-    pairs = columns[..., : heads * 2 * HD].reshape(lead + (heads, 2, HD))
-    values = columns[..., heads * 2 * HD : heads * 3 * HD].reshape(lead + (heads, 1, HD))
-    return jnp.concatenate([pairs, values], axis=-2)
+    wide = heads * 2 * HD + -(-heads // 2) * 2 * HD
+    wanted = np.arange(heads * 3 * HD).reshape(heads, 3, HD)
+    source = np.concatenate([wanted[:, :2].reshape(-1), wanted[:, 2].reshape(-1)])
+    pick = np.zeros((heads * 3 * HD, wide), np.float32)
+    pick[source, np.arange(source.size)] = 1.0
+    return jnp.dot(columns, jnp.asarray(pick, BF16), preferred_element_type=F32).astype(BF16)
 
 
 def on_device(dp_size, parts, tokens, segments, cotangent, ln1_gain, ln1_bias, w_qkv, q_bias, v_bias, w_out, out_bias, ln2_gain, ln2_bias, w_fc1, fc1_bias, w_fc2, fc2_bias):
@@ -787,49 +865,48 @@
     head_cols = w_out.shape[0]
     heads = head_cols // HD
     hidden_cols = w_fc1.shape[1]
-    vecs = jnp.concatenate([ln1_gain, ln1_bias, out_bias, ln2_gain, ln2_bias, fc2_bias, fc2_bias, fc2_bias])
-    vecs = vecs.reshape(8, width).astype(F32)
     out_rows = -(-head_cols // 128) * 128
     out_padded = jnp.pad(w_out, ((0, out_rows - head_cols), (0, 0)))
     qkv = regroup(w_qkv, heads)
-    line = max(qkv.shape[1], hidden_cols)
-    none = jnp.zeros((16 * line,), BF16)
-    pieces = []
-    for h in range(heads):
-        pieces += [q_bias[h * HD : (h + 1) * HD], none[:HD]]
-    pieces += [v_bias, none[: line - 3 * head_cols], fc1_bias, none[: 15 * line - hidden_cols]]
-    bias = jnp.concatenate(pieces).reshape(16, line)
-
-    output, grad_tokens, sum_qkv, sum_out, sum_fc1, sum_fc2, small, late, cls_features = layer(
-        tokens, cotangent, segments.reshape(-1, SEQ), vecs, bias, [qkv, out_padded, w_fc1, w_fc2], dp_size, parts, heads
+    line = max(2 * head_cols, hidden_cols, width)
+
+    def fit(vector):
+        return jnp.pad(vector, (0, line - vector.shape[0]))
+
+    rows = [ln1_gain, ln1_bias, out_bias, ln2_gain, ln2_bias, fc2_bias, jnp.concatenate([q_bias, v_bias]), fc1_bias]
+    bias = jnp.stack([fit(row) for row in rows]).astype(F32)
+
+    output, grad_tokens, sum_qkv, sum_out, sum_fc1, sum_fc2, small, cls_features = layer(
+        tokens, cotangent, segments.reshape(-1, 128), bias, [qkv, out_padded, w_fc1, w_fc2], dp_size, parts, heads
     )
-    sum_qkv = ungroup(sum_qkv, heads).reshape(sum_qkv.shape[0], -1)
-    sum_out = sum_out[:, :head_cols]
     low = dp_size // FAN
 
-    def finish(array):
+    def finish(array, axis):
         if low == 1:
             return array
         groups = [[i * low + j for j in range(low)] for i in range(FAN)]
-        return lax.psum_scatter(array, "dp", scatter_dimension=0, axis_index_groups=groups, tiled=True)
-
-    sum_qkv, sum_out, sum_fc1, sum_fc2 = (finish(a) for a in (sum_qkv, sum_out, sum_fc1, sum_fc2))
-    mixed_sums = ungroup(late[2 : 2 + parts, : qkv.shape[1]], heads)
+        return lax.psum_scatter(array, "dp", scatter_dimension=axis, axis_index_groups=groups, tiled=True)
+
+    sum_qkv, sum_fc1, sum_out, sum_fc2 = (
+        finish(a, 0) for a in (sum_qkv, sum_fc1, sum_out[:, :head_cols], sum_fc2)
+    )
+    start = 10 + parts
+    mixed_sums = small[start : start + parts]
     return (
         output,
         grad_tokens,
         cls_features,
         sum_qkv,
-        mixed_sums[:, :, 0].reshape(-1),
-        mixed_sums[:, :, 2].reshape(-1),
+        mixed_sums[:, :head_cols].reshape(-1),
+        mixed_sums[:, head_cols : 2 * head_cols].reshape(-1),
         sum_out.T,
         small[0],
         sum_fc1,
-        small[8 : 8 + parts, :hidden_cols].reshape(-1),
+        small[10 : 10 + parts, :hidden_cols].reshape(-1),
         sum_fc2.T,
         small[1],
-        late[0],
-        late[1],
+        small[8],
+        small[9],
         small[2],
         small[3],
     )

time: 215 us -> 197 us (0.916)
  Pallas kernels: 181 us -> 170 us
  local copies, waits for them, and re-layouts: 30.8 us -> 21.1 us
  matrix products: 0 us -> 2.35 us
    pallas_call x1, Pallas kernels: 181 us -> 170 us  [layer(): pl.pallas_call(partial(layer_kernel, dp_size, parts, heads), out_shape=[s...]
    unnamed x29 -> x17, local copies, waits for them, and re-layouts: 12.9 us -> 7.09 us
    concatenate x7 -> x0, local copies, waits for them, and re-layouts: 4.76 us -> none  [the longest x5 2.49 us: regroup(): return jnp.concatenate([pairs, values, pad], axis=-1)]
    slice x12 -> x2, local copies, waits for them, and re-layouts: 5.18 us -> 1.63 us  [the longest x1 0.89 us: on_device(): mixed_sums[:, head_cols:2 * head_cols].reshape(-1)]
    another operation x3 -> x9, local copies, waits for them, and re-layouts: 1.35 us -> 4.85 us  [on_device(): bias = jnp.stack([fit(row) for row in rows]).astype(F32)]
    dot_general x0 -> x1, matrix products: none -> 2.35 us  [regroup(): jnp.dot(columns, jnp.asarray(pick, BF16), preferred_element_type=F32)]
where the time goes in v1:
time: 197 us; the launch traced here: 196 us
  Pallas kernels  170 us (86%)
  local copies, waits for them, and re-layouts  21.1 us (11%)
  matrix products  2.35 us (1%)
    pallas_call x1, Pallas kernels, layer(): pl.pallas_call(partial(layer_kernel, dp_size, parts, heads), out_shape=[s...  170 us
    unnamed x17, local copies, waits for them, and re-layouts  7.09 us
    another operation x9, local copies, waits for them, and re-layouts, on_device(): bias = jnp.stack([fit(row) for row in rows]).astype(F32)  4.85 us

profile of v1, /device:TPU:0, one launch (start us, length us, event | category | flops | bytes accessed | tf_op | source)
XLA Modules:
  0.0 195.9 jit_solution(18361924215505576214)
XLA Ops:
  0.6 0.7 fusion.3
  1.4 0.7 stack.27
  2.1 0.7 stack.28
  2.8 0.7 stack.29
  3.5 0.7 stack.30
  4.1 0.7 stack.31
  4.8 0.7 stack.34
  5.5 0.7 stack.32
  6.2 0.6 convert_element_type.10.refs_3_.refs_4_
  6.9 1.7 pad.9
  8.6 2.4 %fusion = bf16[768,640]{0,1:T(8,128)(2,1)S(1)} fusion(bf16[576,640]{1,0:T(8,128)(2,1)} %constant.5.clone, bf16[768,576]{0,1:T(8,128)(2,1)} %param.22), kind=kOutput, calls=%fused_computation.1 | convolution fusion | flops 566722560 | bytes 2605056 | tf_op jit(solution)/shard_map/dot_general | solution.py:859
  11.0 1.3 copy.33
  12.3 170.4 %shard_map.288 = (bf16[512,768]{1,0:T(8,128)(2,1)}, bf16[512,768]{1,0:T(8,128)(2,1)}, f32[96,576]{1,0:T(8,128)}, f32[96,256]{1,0:T(8,128)}, f32[96,768]{1,0:T(8,...) custom-call(bf16[512,768]{1,0:T(8,128)(2,1)} %refs_0_.1, bf16[512,768]{1,0:T(8,128)(2,1)} %refs_1_.1, ...), custom_call_target="tpu_custom_call" | custom-call | tf_op jit(solution)/shard_map/pallas_call | solution.py:839
  182.7 0.0 copy-start.1
  182.7 0.9 fusion.4
  183.6 0.7 reshape.62
  184.3 0.7 reshape.61
  185.0 0.7 slice.37
  185.7 1.6 slice_reduce_fusion
  187.3 0.6 reshape.63
  187.9 0.9 slice_bitcast_fusion
  188.8 0.7 copy.34
  189.6 0.0 copy-start
  189.6 2.2 %copy.41 = bf16[512,768]{1,0:T(8,128)(2,1)} copy(bf16[512,768]{1,0:T(8,128)(2,1)} %get-tuple-element.72) | data formatting | bytes 1572864
  191.7 0.0 copy-done.1
  191.7 0.9 copy.42
  192.6 0.0 copy-done
  192.6 0.0 copy-start.4
  192.6 0.0 copy-start.3
  192.6 0.0 copy-start.2
  192.6 1.1 copy.43
  193.8 0.0 copy-done.4
  193.8 0.7 copy.44
  194.5 0.0 copy-done.3
  194.5 0.7 copy.45
  195.2 0.0 copy-done.2
  195.2 0.7 copy.46
  (2 shorter events, 0.1 us)
Async XLA Ops:
  182.7 9.0 %copy-start.1 = (bf16[512,768]{1,0:T(8,128)(2,1)S(1)}, bf16[512,768]{1,0:T(8,128)(2,1)}, u32[]{:S(2)}) copy-start(bf16[512,768]{1,0:T(8,128)(2,1)} %get-tuple-element.73) | copy-start | bytes 2359300
  189.6 3.1 %copy-start = (f32[512,768]{1,0:T(8,128)S(1)}, f32[512,768]{1,0:T(8,128)}, u32[]{:S(2)}) copy-start(f32[512,768]{1,0:T(8,128)} %get-tuple-element.74) | copy-start | bytes 4718596
  192.6 1.2 copy-start.4
  192.6 1.9 copy-start.3
  192.6 2.6 %copy-start.2 = (f32[96,768]{1,0:T(8,128)S(1)}, f32[96,768]{1,0:T(8,128)}, u32[]{:S(2)}) copy-start(f32[96,768]{1,0:T(8,128)} %get-tuple-element.31) | copy-start | bytes 884740

commit v2 on v1

--- a/solution.py
+++ b/solution.py
@@ -146,6 +146,7 @@
 class Gather:
     def __init__(self, here, along, relay, later):
         self.t, self.along, self.relay, self.later = here.t, along, relay, later
+        self.extra = []
 
     def guarded(self, what, does):
         if self.relay is None:
@@ -157,8 +158,6 @@
         pl.when(ends[0])(lambda: does(up))
         does(across)
         pl.when(ends[1])(lambda: does(down))
-        for made in self.along[3:]:
-            does(made)
 
     def relayed(self, what, does):
         up, down = self.relay
@@ -172,6 +171,7 @@
     def step(self, s):
         if s == "z":
             self.guarded("in", lambda made: made.wait_recv())
+            arrive(self.extra)
             if self.relay is not None:
                 self.relayed("out", lambda made: made.start())
             return
@@ -187,7 +187,7 @@
         self.guarded("out", lambda made: made.wait_send())
         if self.relay is not None:
             self.relayed("out", lambda made: made.wait_send())
-        for copies in self.later:
+        for copies in self.later + [self.extra]:
             left(copies)
 
 
@@ -255,14 +255,28 @@
     ) * scale
 
 
+def select(values, pick):
+    high = values.astype(BF16)
+    rest = values - high.astype(F32)
+    middle = rest.astype(BF16)
+    low = (rest - middle.astype(F32)).astype(BF16)
+    return mm(high, pick) + mm(middle, pick) + mm(low, pick)
+
+
 ROWS = 64
 UNITS = 5
 NAMES = (
     "tokens",
     "cot",
     "segments",
-    "vecs",
-    "bias",
+    "ln1_gain",
+    "ln1_bias",
+    "out_bias",
+    "ln2_gain",
+    "ln2_bias",
+    "fc2_bias",
+    "qv_bias",
+    "fc1_bias",
     "w_qkv",
     "w_out",
     "w_fc1",
@@ -314,7 +328,7 @@
     got = [[refs.pop(0) for _ in range(5)] for _ in range(UNITS + parts)]
     got_z = [refs.pop(0) for _ in range(UNITS + 1)]
     local_sem, send_sem, recv_sem = refs
-    tokens, cot, cols, vecs = ref["tokens"], ref["cot"], ref["cols"], ref["vecs"]
+    tokens, cot, cols, vecs = ref["tokens"], ref["cot"], ref["cols"], ref["biases"].at[0]
     segments = ref["segments"]
     f_qkv, f_out, f_fc1, f_fc2 = ref["f_qkv"], ref["f_out"], ref["f_fc1"], ref["f_fc2"]
     biases, normed, mixed, mask = ref["biases"], ref["normed"], ref["mixed"], ref["mask"]
@@ -338,23 +352,35 @@
     shards = [ref[n] for n in ("w_qkv", "w_out", "w_fc1", "w_fc2")]
     wholes = [f_qkv, f_out, f_fc1, f_fc2]
     own = [
-        pltpu.make_async_copy(a, b.at[0], local_sem.at[i])
-        for i, (a, b) in enumerate(zip(shards + [ref["bias"]], wholes + [biases]))
+        pltpu.make_async_copy(shards[i], wholes[i].at[0], local_sem.at[i]) for i in (0, 2, 3)
     ]
-    start(own)
+    blocks = shards[1].shape[0]
+    places = [f_out.at[0, b // 4, (b // 2) % 2, b % 2] for b in range(FAN)]
+    own_out = [
+        pltpu.make_async_copy(shards[1].at[b], places[b], local_sem.at[4 + b]) for b in range(blocks)
+    ]
+    start(own_out + own)
+    for b in range(blocks, FAN):
+        places[b][...] = jnp.zeros_like(places[b])
+    for i, name in enumerate(NAMES[3:11]):
+        lanes = ref[name][...].astype(F32)
+        for b in range(lanes.shape[0]):
+            vecs[i : i + 1, pl.ds(b * 128, 128)] = lanes[b : b + 1]
     greet(bits + [here.shift(k) for k in range(1, parts)])
     def columns(array, first, many):
         return array.at[:, :, :, :, pl.ds(first, many)] if len(array.shape) == 5 else array.at[:, :, :, :, :, pl.ds(first, many)]
 
     cut = f_fc1.shape[5] // 2
-    plans = {"q": gather_unit(here, link, shards[0], f_qkv), "o": gather_unit(here, link, shards[1], f_out)}
+    plans = {"q": gather_unit(here, link, shards[0], f_qkv), "o": gather_unit(here, link, f_out.at[0], f_out)}
     for name, i, first in (("a", 2, 0), ("b", 2, cut), ("c", 3, 0), ("d", 3, cut)):
         plans[name] = gather_unit(
             here, link, columns(shards[i], first, cut), columns(wholes[i], first, cut)
         )
-    plans["q"].along += [
-        link.copy(ref["bias"], biases.at[parts - k], here.shift(k)) for k in range(1, parts)
+    plans["q"].extra = [
+        link.copy(biases.at[0], biases.at[parts - k], here.shift(k)) for k in range(1, parts)
     ]
+    for made in own_out:
+        made.wait()
     for name in "qoa":
         plans[name].begin()
     units = {}
@@ -364,10 +390,10 @@
             ("B", columns(g_fc2, cut, cut)),
             ("C", columns(g_fc1, 0, cut)),
             ("D", columns(g_fc1, cut, cut)),
-            ("O", g_out),
         )
     ):
         units[name] = Reduction(here, link, grad, 0, parts, got[i], got_z[i])
+    units["O"] = Reduction(here, link, g_out, 0, parts, got[UNITS - 1], got_z[UNITS - 1])
     for k in range(parts):
         units[k] = Reduction(here, link, g_qkv, k, 1, got[UNITS + k], got_z[UNITS])
 
@@ -441,6 +467,7 @@
         mask[r, :] = jnp.where(cols[r, 0:1] == line, 0.0, -1e30)
 
     loop(chunks, norm_one)
+    start(plans["q"].extra)
 
     low_half = lax.broadcasted_iota(jnp.int32, (SEQ, 128), 1) < 64
 
@@ -491,7 +518,6 @@
         hd[k, :, h_at] = jnp.where(mine_of(even), out, before).astype(BF16)
 
     own[0].wait()
-    own[4].wait()
     qkv_part(0)
     loop(heads, attend, {1: fwd(("q", "z"))})
     fwd(("o", "z"), ("b", "go"), ("q", 0), ("o", 0))()
@@ -502,17 +528,13 @@
         heads * (parts - 1),
         lambda i: attend(i + heads),
         {
-            1: fwd(("o", 2), ("c", 0), ("d", "z")),
-            2: fwd(("b", 1), ("d", 0)),
-            3: fwd(("a", 2)),
-            4: fwd(("o", 3)),
-            5: fwd(("c", 1)),
-            6: fwd(("b", 2), ("a", 3)),
-            7: fwd(("d", 1)),
-            8: fwd(("c", 2)),
+            0: fwd(("o", 2), ("c", 0)),
+            1: fwd(("b", 1), ("d", "z")),
+            2: fwd(("d", 0)),
+            5: fwd(("a", 2), ("o", 3)),
         },
     )
-    for made in own[1:4]:
+    for made in own[1:]:
         made.wait()
 
     def project(n):
@@ -523,6 +545,7 @@
         resid[:, at] = total
 
     loop(width // 256, project)
+    fwd(("b", 2), ("a", 3))()
 
     def norm_two(i):
         r = rows_of(i)
@@ -530,6 +553,7 @@
         normed2[r, :] = (hat * gain(3) + gain(4)).astype(BF16)
 
     loop(chunks, norm_two)
+    fwd(("c", 1))()
     hid = f_fc1.shape[5]
     tiles = hid // 256
 
@@ -551,11 +575,11 @@
         loop(chunks, gelu)
 
     loop(tiles, fc1_tile)
-    fwd(("b", 3))()
+    fwd(("b", 3), ("d", 1))()
     loop(
         tiles * (parts - 1),
         lambda i: fc1_tile(i + tiles),
-        {2: fwd(("d", 2)), 4: fwd(("c", 3))},
+        {7: fwd(("c", 2))},
     )
 
     def grad_branch(i):
@@ -587,7 +611,7 @@
     small[1:2, :] = mm(ones, g_low[...])[0:1]
     loop(parts, weight_grad(g_fc2, active, hid))
     red(("A", 0), ("B", 0))()
-    fwd(("d", 3))()
+    fwd(("d", 2), ("c", 3), ("d", 3))()
     for plan in plans.values():
         plan.drain()
 
@@ -603,8 +627,7 @@
         small[4:5, at] = jnp.sum(picked, axis=0, keepdims=True)
         small[5:6, at] = jnp.sum(picked * values, axis=0, keepdims=True)
 
-    loop(width // 256, finish, {2: red(("A", 1))})
-    red(("B", 1))()
+    loop(width // 256, finish, {1: red(("A", 1)), 2: red(("B", 1))})
     small[6:7, :] = jnp.broadcast_to(jnp.sum(cols[:, 2:3], axis=0, keepdims=True), (1, width))
     side = hid // 2
 
@@ -741,7 +764,7 @@
     for k in range(parts):
         red((k, 3))()
     small_round(2)
-    total(g_out, got_z[4], ref["s_out"])
+    total(g_out, got_z[UNITS - 1], ref["s_out"])
     for r in range(3, len(trips) + 1):
         small_round(r)
     for i, first in enumerate((0, cut)):
@@ -753,14 +776,8 @@
     target = lax.broadcasted_iota(jnp.int32, (wide, heads * triple), 1)
     head, lane = target // triple, target % triple
     wanted = jnp.where(lane < 2 * HD, head * 2 * HD + lane, qk_wide + head * HD + lane - 2 * HD)
-    unpick = jnp.where(source == wanted, 1.0, 0.0)
-    ref["s_qkv"][...] = lax.dot_general(
-        total(g_qkv, got_z[UNITS]),
-        unpick,
-        (((1,), (0,)), ((), ())),
-        precision=lax.Precision.HIGHEST,
-        preferred_element_type=F32,
-    )
+    unpick = jnp.where(source == wanted, 1.0, 0.0).astype(BF16)
+    ref["s_qkv"][...] = select(total(g_qkv, got_z[UNITS]), unpick)
     arrive(spread_out)
     final = all_sums[0]
     for t in range(1, parts):
@@ -771,12 +788,8 @@
     wanted = jnp.where(
         target < head_cols, (target // HD) * 2 * HD + target % HD, qk_wide + target - head_cols
     )
-    ref["small"][pl.ds(10 + parts, parts), pl.ds(0, 2 * head_cols)] = lax.dot_general(
-        final[:, :wide],
-        jnp.where(source == wanted, 1.0, 0.0),
-        (((1,), (0,)), ((), ())),
-        precision=lax.Precision.HIGHEST,
-        preferred_element_type=F32,
+    ref["small"][pl.ds(10 + parts, parts), pl.ds(0, 2 * head_cols)] = select(
+        final[:, :wide], jnp.where(source == wanted, 1.0, 0.0).astype(BF16)
     )[10 + parts : 10 + 2 * parts]
     mean = final[4:5, :] / final[6:7, :]
     spread = final[5:6, :] / final[6:7, :] - mean * mean
@@ -792,18 +805,23 @@
         unit.drain()
 
 
-def layer(tokens, cot, segments, bias, shards, dp_size, parts, heads):
-    shards = [s.reshape(2, 2, 2, s.shape[0] // FAN, s.shape[1]) for s in shards]
-    width, hid = tokens.shape[1], shards[2].shape[4]
-    wide, v_wide = shards[0].shape[4], FAN * shards[1].shape[3]
+def layer(tokens, cot, segments, vectors, shards, dp_size, parts, heads):
+    width, hid, wide = tokens.shape[1], shards[2].shape[1], shards[0].shape[1]
+    v_wide = -(-heads // 2) * 2 * HD
+    piece = v_wide // FAN
+    whole = [pltpu.VMEM((parts, 2, 2, 2, rows // FAN, n), BF16) for rows, n in ((width, wide), (v_wide, width), (width, hid), (hid, width))]
+    shards = [
+        s.reshape(-1, piece, width) if i == 1 else s.reshape(2, 2, 2, s.shape[0] // FAN, s.shape[1])
+        for i, s in enumerate(shards)
+    ]
+    line = max(v.shape[0] for v in vectors)
     lines = -(-(10 + 2 * parts) // 8) * 8
     rounds = dp_size.bit_length() - 1
     copies = 6 * (5 + parts + 1) + parts - 1 + (UNITS + parts) * (5 + parts) + rounds + parts
     blk = width // FAN
     grads = [(blk, wide), (blk, v_wide), (blk, hid), (blk, hid)]
-    whole = [pltpu.VMEM((parts,) + s.shape, BF16) for s in shards]
     scratch = whole + [
-        pltpu.VMEM((parts,) + bias.shape, F32),
+        pltpu.VMEM((parts, len(vectors), line), F32),
         pltpu.VMEM((SEQ, width), BF16),
         pltpu.VMEM((parts, SEQ, wide), BF16),
         pltpu.VMEM((SEQ, SEQ), F32),
@@ -831,7 +849,7 @@
     for _, n in sizes[: UNITS + 1]:
         scratch.append(pltpu.VMEM((parts - 1, blk, n), BF16))
     scratch += [
-        pltpu.SemaphoreType.DMA((5,)),
+        pltpu.SemaphoreType.DMA((4 + FAN,)),
         pltpu.SemaphoreType.DMA((copies,)),
         pltpu.SemaphoreType.DMA((copies,)),
     ]
@@ -841,13 +859,13 @@
         out_shape=[shape(tokens.shape, BF16), shape(tokens.shape, BF16)]
         + [shape((blk, heads * 3 * HD), F32), shape((blk, v_wide), F32), shape((blk, hid), F32), shape((blk, hid), F32)]
         + [shape((lines, width), F32), shape(tokens.shape, F32)],
-        in_specs=[VMEM] * 4 + [ANY] * 5,
+        in_specs=[VMEM] * (3 + len(vectors)) + [ANY] * 4,
         out_specs=[VMEM] * 8,
         scratch_shapes=scratch,
         compiler_params=pltpu.CompilerParams(
             collective_id=0, has_side_effects=True, vmem_limit_bytes=67043328
         ),
-    )(tokens, cot, segments, bias, bias, *shards)
+    )(tokens, cot, segments, *[v.reshape(-1, 128) for v in vectors], *shards)
 
 
 def regroup(columns, heads):
@@ -865,19 +883,11 @@
     head_cols = w_out.shape[0]
     heads = head_cols // HD
     hidden_cols = w_fc1.shape[1]
-    out_rows = -(-head_cols // 128) * 128
-    out_padded = jnp.pad(w_out, ((0, out_rows - head_cols), (0, 0)))
     qkv = regroup(w_qkv, heads)
-    line = max(2 * head_cols, hidden_cols, width)
-
-    def fit(vector):
-        return jnp.pad(vector, (0, line - vector.shape[0]))
-
-    rows = [ln1_gain, ln1_bias, out_bias, ln2_gain, ln2_bias, fc2_bias, jnp.concatenate([q_bias, v_bias]), fc1_bias]
-    bias = jnp.stack([fit(row) for row in rows]).astype(F32)
+    vectors = [ln1_gain, ln1_bias, out_bias, ln2_gain, ln2_bias, fc2_bias, jnp.concatenate([q_bias, v_bias]), fc1_bias]
 
     output, grad_tokens, sum_qkv, sum_out, sum_fc1, sum_fc2, small, cls_features = layer(
-        tokens, cotangent, segments.reshape(-1, 128), bias, [qkv, out_padded, w_fc1, w_fc2], dp_size, parts, heads
+        tokens, cotangent, segments.reshape(-1, 128), vectors, [qkv, w_out, w_fc1, w_fc2], dp_size, parts, heads
     )
     low = dp_size // FAN
 

time: 197 us -> 190 us (0.964)
  local copies, waits for them, and re-layouts: 21.1 us -> 14.5 us
    another operation x9 -> x0, local copies, waits for them, and re-layouts: 4.85 us -> none  [on_device(): bias = jnp.stack([fit(row) for row in rows]).astype(F32)]
where the time goes in v2:
time: 190 us; the launch traced here: 189 us
  Pallas kernels  170 us (89%)
  local copies, waits for them, and re-layouts  14.5 us (8%)
  matrix products  2.35 us (1%)
    pallas_call x1, Pallas kernels, layer(): pl.pallas_call(partial(layer_kernel, dp_size, parts, heads), out_shape=[s...  170 us
    unnamed x17, local copies, waits for them, and re-layouts  7.09 us

profile of v2, /device:TPU:0, one launch (start us, length us, event | category | flops | bytes accessed | tf_op | source)
XLA Modules:
  0.0 189.2 jit_solution(210295262837207007)
XLA Ops:
  0.6 1.3 maximum_bitcast_fusion.refs_9_
  2.0 2.4 %fusion = bf16[768,640]{0,1:T(8,128)(2,1)S(1)} fusion(bf16[576,640]{1,0:T(8,128)(2,1)} %constant.2.clone, bf16[768,576]{0,1:T(8,128)(2,1)} %param.22), kind=kOutput, calls=%fused_computation.1 | convolution fusion | flops 566722560 | bytes 2605056 | tf_op jit(solution)/shard_map/dot_general | solution.py:877
  4.3 1.3 copy.33
  5.6 170.4 %shard_map.288 = (bf16[512,768]{1,0:T(8,128)(2,1)}, bf16[512,768]{1,0:T(8,128)(2,1)}, f32[96,576]{1,0:T(8,128)}, f32[96,256]{1,0:T(8,128)}, f32[96,768]{1,0:T(8,...) custom-call(bf16[512,768]{1,0:T(8,128)(2,1)} %refs_0_.1, bf16[512,768]{1,0:T(8,128)(2,1)} %refs_1_.1, ...), custom_call_target="tpu_custom_call" | custom-call | tf_op jit(solution)/shard_map/pallas_call | solution.py:857
  176.0 0.0 copy-start.1
  176.0 0.9 fusion.1
  176.9 0.7 reshape.94
  177.6 0.7 reshape.93
  178.3 0.7 slice.37
  179.0 1.6 slice_reduce_fusion
  180.6 0.6 reshape.95
  181.2 0.9 slice_bitcast_fusion
  182.1 0.7 copy.34
  182.9 0.0 copy-start
  182.9 2.2 %copy.41 = bf16[512,768]{1,0:T(8,128)(2,1)} copy(bf16[512,768]{1,0:T(8,128)(2,1)} %get-tuple-element.72) | data formatting | bytes 1572864
  185.0 0.0 copy-done.1
  185.0 0.9 copy.42
  185.9 0.0 copy-done
  185.9 0.0 copy-start.4
  185.9 0.0 copy-start.3
  185.9 0.0 copy-start.2
  185.9 1.1 copy.43
  187.1 0.0 copy-done.4
  187.1 0.7 copy.44
  187.8 0.0 copy-done.3
  187.8 0.7 copy.45
  188.5 0.0 copy-done.2
  188.5 0.7 copy.46
Async XLA Ops:
  176.0 9.0 %copy-start.1 = (bf16[512,768]{1,0:T(8,128)(2,1)S(1)}, bf16[512,768]{1,0:T(8,128)(2,1)}, u32[]{:S(2)}) copy-start(bf16[512,768]{1,0:T(8,128)(2,1)} %get-tuple-element.73) | copy-start | bytes 2359300
  182.9 3.1 %copy-start = (f32[512,768]{1,0:T(8,128)S(1)}, f32[512,768]{1,0:T(8,128)}, u32[]{:S(2)}) copy-start(f32[512,768]{1,0:T(8,128)} %get-tuple-element.74) | copy-start | bytes 4718596
  185.9 1.2 copy-start.4
  185.9 1.9 copy-start.3
  185.9 2.6 %copy-start.2 = (f32[96,768]{1,0:T(8,128)S(1)}, f32[96,768]{1,0:T(8,128)}, u32[]{:S(2)}) copy-start(f32[96,768]{1,0:T(8,128)} %get-tuple-element.31) | copy-start | bytes 884740
